TPU v7x, 32 devices: a whole 2x2x4 slice. The times are simulated.
32 devices in a mesh: agent: 16 (over z, y, x), grid: 2 (over core).
Axes of the slice: x: 2, y: 2, z: 4, core: 2. Of those that a mesh axis runs over, the one named last changes fastest.
Arguments:
- value_prior: float32 [2048, 1024], P(None, 'agent'), may hold values from -6 to 6
- trans_weight: float32 [128, 128], replicated, may hold values from 0.05 to 1
- perceived_law_coefficient: float32 [4], replicated, may hold values from 0.7 to 1
- perceived_law_constant: float32 [4], replicated, may hold values from 0.5 to 4
- interest: float32 [4, 16], replicated, may hold values from 0 to 0.05
- wage_level: float32 [4, 16], replicated, may hold values from 0.5 to 1.5
- efficiency: float32 [32], replicated, may hold values from 0.2 to 3
- holdings: float32 [131072], P('agent'), may hold values from 0 to 40
- shocks: int32 [4, 131072], P(None, 'agent'), may hold values from 0 to 31
- brackets: int32 [4, 131072], P(None, 'agent'), may hold values from 0 to 1022
- aggregate: int32 [4], replicated, may hold values from 0 to 3
Outputs:
- value_new: float32 [2048, 1024], P('agent', 'grid')
- policy: float32 [2048, 1024], P('agent', 'grid')
- holdings_final: float32 [131072], P('agent')
- capital: float32 [4], replicated
All inputs are finite; a program needn't handle non-finite values.
Results may differ from a plain program's by a relative error of at most 0.0003.
Values sent between devices are 32-bit elements; how exact they have to be, the bound alone decides.
A program may use at most 64 MiB of HBM per device.

v0:
```python
import jax
import jax.numpy as jnp
from jax import lax
from jax.sharding import PartitionSpec as P

A = 1024
E = 32
NK = 16
Z = 4
STATES = 2048
PERIODS = 4


wealth_upper_limit = 40.0
beta_disc = 0.96
tau_soft = 0.02
floor_cons = 0.1
highest = lax.Precision.HIGHEST


def make_points():
    fraction = jnp.arange(A, dtype=jnp.float32) / (A - 1)
    return wealth_upper_limit * fraction * fraction


def hat_function_shares(position):
    spacing = wealth_upper_limit / (NK - 1)
    savings_mesh_points = wealth_upper_limit * jnp.arange(NK, dtype=jnp.float32) / (NK - 1)
    return jnp.maximum(0.0, 1.0 - jnp.abs(position[..., None] - savings_mesh_points) / spacing)


def one_hot(indices, number):
    return (indices[:, None] == jnp.arange(number, dtype=jnp.int32)[None, :]).astype(jnp.float32)


def state_parts(states):
    zone_of = states // (NK * E)
    level_of = states // E % NK
    kind_of = states % E
    return (zone_of, level_of, kind_of)


def expect_rows(rows_in, transition, offset_coefficients):
    columns = rows_in.shape[1]
    value_cube = rows_in.reshape(Z, NK, E, columns)
    blended = jnp.einsum(
        "zeyf,ykfn->zekn", transition.reshape(Z, E, Z, E), value_cube, precision=highest
    )
    result = jnp.einsum("zjk,zekn->zjen", offset_coefficients, blended, precision=highest)
    return result.reshape(STATES, columns)


def bellman(points, wealth, expected):
    consume = wealth[:, None] - points[None, :]
    clipped = jnp.maximum(consume, floor_cons)
    utility = jnp.log(clipped) + (consume - clipped) / floor_cons
    scores = (utility + beta_disc * expected[None, :]) / tau_soft
    highest_score = jnp.max(scores, axis=1, keepdims=True)
    weight = jnp.exp(scores - highest_score)
    totals = jnp.sum(weight, axis=1)
    values_now = tau_soft * (highest_score[:, 0] + jnp.log(totals))
    chosen = jnp.sum(weight * points[None, :], axis=1) / totals
    return (values_now, chosen)


def advance(lookup, points, current, shock_row, bracket_row):
    flattened = lookup.reshape(-1)
    flat_index = shock_row * lookup.shape[1] + bracket_row
    value_low = jnp.take(flattened, flat_index)
    value_high = jnp.take(flattened, flat_index + 1)
    edge_low = jnp.take(points, bracket_row)
    edge_high = jnp.take(points, bracket_row + 1)
    fraction = jnp.clip((current - edge_low) / (edge_high - edge_low), 0.0, 1.0)
    return value_low + fraction * (value_high - value_low)


def on_device(
    value_prior,
    trans_weight,
    perceived_law_coefficient,
    perceived_law_constant,
    interest,
    wage_level,
    efficiency,
    holdings,
    shocks,
    brackets,
    aggregate,
):
    agent_count = lax.axis_size("agent")
    per_device = STATES // agent_count
    half_rows = A // lax.axis_size("grid")
    first_state = lax.axis_index("agent") * per_device
    own_states = first_state + jnp.arange(per_device, dtype=jnp.int32)
    points = make_points()
    transition = trans_weight / jnp.sum(trans_weight, axis=1, keepdims=True)
    savings_mesh_points = wealth_upper_limit * jnp.arange(NK, dtype=jnp.float32) / (NK - 1)
    predicted_stock = jnp.clip(
        perceived_law_coefficient[:, None] * savings_mesh_points[None, :]
        + perceived_law_constant[:, None],
        0.0,
        wealth_upper_limit,
    )
    offset_coefficients = hat_function_shares(predicted_stock)
    partial_value = expect_rows(value_prior, transition, offset_coefficients)
    expected = lax.all_to_all(partial_value, "agent", split_axis=0, concat_axis=1, tiled=True)
    zone_of, level_of, kind_of = state_parts(own_states)
    price_hot = one_hot(zone_of * NK + level_of, Z * NK)
    interest_own = jnp.sum(price_hot * interest.reshape(1, Z * NK), axis=1)
    wage_own = jnp.sum(price_hot * wage_level.reshape(1, Z * NK), axis=1)
    kind_hot = one_hot(kind_of, E)
    efficiency_own = jnp.sum(kind_hot * efficiency[None, :], axis=1)
    growth = 1.0 + interest_own
    income = wage_own * efficiency_own
    own_points = lax.dynamic_slice_in_dim(points, lax.axis_index("grid") * half_rows, half_rows)

    def one_state(packed):
        column, factor, earned = packed
        return bellman(points, own_points * factor + earned, column)

    values_now, policy = lax.map(one_state, (expected, growth, income))
    agents_total = holdings.shape[0] * agent_count
    halves_in = lax.all_gather(policy, "grid", axis=1, tiled=True)
    policy_cube = lax.all_gather(halves_in, "agent", axis=0, tiled=True).reshape(Z, NK, E, A)
    current = holdings
    capital_path = []
    for period in range(PERIODS):
        capital = lax.psum(jnp.sum(current), "agent") / agents_total
        capital_path.append(capital)
        knot_weights = hat_function_shares(capital)
        sliced = lax.dynamic_index_in_dim(policy_cube, aggregate[period], 0, keepdims=False)
        lookup = jnp.einsum("k,kea->ea", knot_weights, sliced, precision=highest)
        current = advance(lookup, points, current, shocks[period], brackets[period])
    return (values_now, policy, current, jnp.stack(capital_path))


def solution(mesh):
    return jax.shard_map(
        on_device,
        mesh=mesh,
        in_specs=(
            P(None, "agent"),
            P(),
            P(),
            P(),
            P(),
            P(),
            P(),
            P("agent"),
            P(None, "agent"),
            P(None, "agent"),
            P(),
        ),
        out_specs=(P("agent", "grid"), P("agent", "grid"), P("agent"), P()),
        check_vma=False,
    )
```

profile of v0, /device:TPU:0, one launch (start us, length us, event | category | flops | bytes accessed | tf_op | source)
XLA Modules:
  0.0 1654.3 jit_solution(14126307934006875901)
XLA Ops:
  7.2 1.4 copy.26
  11.9 1.5 fusion.10
  14.8 8.3 all-to-all-start
  23.8 14.5 all-to-all-done
  38.5 789.8 %while.14 = (s32[]{:T(128)}, f32[128,512]{1,0:T(8,128)}, f32[128,512]{1,0:T(8,128)S(1)}, f32[128]{0:T(128)S(1)}, f32[512]{0:T(512)S(1)}, /*index=5*/f32[128]{0:T...) while((s32[]{:T(128)}, f32[128,512]{1,0:T(8,128)}, f32[128,512]{1,0:T(8,128)S(1)}, ...), condition=%wide.region_8.9_spmd.clone.clone, body=%wide.region_4.8_spmd.clone.clone.sunk | while | flops 9966594 | bytes 63633 | solution.py:121
  41.9 1.4 multiply_reduce_fusion.2
  48.1 1.4 multiply_reduce_fusion.2
  54.3 1.4 multiply_reduce_fusion.2
  60.4 1.4 multiply_reduce_fusion.2
  66.6 1.4 multiply_reduce_fusion.2
  72.8 1.4 multiply_reduce_fusion.2
  78.9 1.4 multiply_reduce_fusion.2
  85.1 1.4 multiply_reduce_fusion.2
  91.3 1.4 multiply_reduce_fusion.2
  97.5 1.4 multiply_reduce_fusion.2
  103.6 1.4 multiply_reduce_fusion.2
  109.8 1.4 multiply_reduce_fusion.2
  116.0 1.4 multiply_reduce_fusion.2
  122.1 1.4 multiply_reduce_fusion.2
  128.3 1.4 multiply_reduce_fusion.2
  134.5 1.4 multiply_reduce_fusion.2
  140.6 1.4 multiply_reduce_fusion.2
  146.8 1.4 multiply_reduce_fusion.2
  153.0 1.4 multiply_reduce_fusion.2
  159.2 1.4 multiply_reduce_fusion.2
  165.3 1.4 multiply_reduce_fusion.2
  171.5 1.4 multiply_reduce_fusion.2
  177.7 1.4 multiply_reduce_fusion.2
  183.8 1.4 multiply_reduce_fusion.2
  190.0 1.4 multiply_reduce_fusion.2
  196.2 1.4 multiply_reduce_fusion.2
  202.3 1.4 multiply_reduce_fusion.2
  208.5 1.4 multiply_reduce_fusion.2
  214.7 1.4 multiply_reduce_fusion.2
  220.9 1.4 multiply_reduce_fusion.2
  227.0 1.4 multiply_reduce_fusion.2
  233.2 1.4 multiply_reduce_fusion.2
  239.4 1.4 multiply_reduce_fusion.2
  828.3 2.3 all_gather.6
  831.3 41.0 %psum.28 = f32[]{:T(128)} all-reduce(f32[]{:T(128)} %reduce_sum.94), channel_id=1, replica_groups=mesh['agent'=16,'grid'=2] {'agent'}, use_global_device_ids=true, to_apply=%region_10.11 | all-reduce | flops 1 | bytes 8 | tf_op jit(solution)/shard_map/psum | solution.py:128
  878.2 32.9 %gather_fusion.2 = f32[8192]{0:T(1024)S(1)} fusion(f32[1024]{0:T(1024)S(1)} %fusion.57, s32[8192]{0:T(1024)S(1)} %get-tuple-element.165), kind=kCustom, calls=%fused_computation.9.clone | custom fusion | bytes 98304 | tf_op jit(solution)/shard_map/jit(_take)/gather | solution.py:72
  911.1 32.9 %gather_fusion.1 = f32[8192]{0:T(1024)S(1)} fusion(f32[1024]{0:T(1024)S(1)} %fusion.57, s32[8192]{0:T(1024)S(1)} %get-tuple-element.166), kind=kCustom, calls=%fused_computation.1.clone | custom fusion | bytes 98304 | tf_op jit(solution)/shard_map/jit(_take)/gather | solution.py:71
  944.0 32.9 %gather_fusion.6 = f32[8192]{0:T(1024)S(1)} fusion(f32[1024]{0:T(1024)S(1)} %fusion.57, s32[8192]{0:T(1024)S(1)} %get-tuple-element.163), kind=kCustom, calls=%fused_computation.11.clone | custom fusion | bytes 98304 | tf_op jit(solution)/shard_map/jit(_take)/gather | solution.py:72
  976.9 32.9 %gather_fusion.5 = f32[8192]{0:T(1024)S(1)} fusion(f32[1024]{0:T(1024)S(1)} %fusion.57, s32[8192]{0:T(1024)S(1)} %get-tuple-element.164), kind=kCustom, calls=%fused_computation.10.clone | custom fusion | bytes 98304 | tf_op jit(solution)/shard_map/jit(_take)/gather | solution.py:71
  1009.8 32.9 %gather_fusion.10 = f32[8192]{0:T(1024)S(1)} fusion(f32[1024]{0:T(1024)S(1)} %fusion.57, s32[8192]{0:T(1024)S(1)} %get-tuple-element.161), kind=kCustom, calls=%fused_computation.13.clone | custom fusion | bytes 98304 | tf_op jit(solution)/shard_map/jit(_take)/gather | solution.py:72
  1042.7 32.9 %gather_fusion.9 = f32[8192]{0:T(1024)S(1)} fusion(f32[1024]{0:T(1024)S(1)} %fusion.57, s32[8192]{0:T(1024)S(1)} %get-tuple-element.162), kind=kCustom, calls=%fused_computation.12.clone | custom fusion | bytes 98304 | tf_op jit(solution)/shard_map/jit(_take)/gather | solution.py:71
  1075.6 32.9 %gather_fusion.14 = f32[8192]{0:T(1024)S(1)} fusion(f32[1024]{0:T(1024)S(1)} %fusion.57, s32[8192]{0:T(1024)S(1)} %get-tuple-element.158), kind=kCustom, calls=%fused_computation.15.clone | custom fusion | bytes 98304 | tf_op jit(solution)/shard_map/jit(_take)/gather | solution.py:72
  1108.5 32.9 %gather_fusion.13 = f32[8192]{0:T(1024)S(1)} fusion(f32[1024]{0:T(1024)S(1)} %fusion.57, s32[8192]{0:T(1024)S(1)} %get-tuple-element.157), kind=kCustom, calls=%fused_computation.14.clone | custom fusion | bytes 98304 | tf_op jit(solution)/shard_map/jit(_take)/gather | solution.py:71
  1144.6 4.5 constant_dynamic-slice_fusion.3
  1150.3 2.6 copy.40
  1152.8 2.5 copy.39
  1157.7 45.5 %gather_fusion.3 = f32[8192]{0:T(1024)S(1)} fusion(f32[32768]{0:T(1024)S(1)} %bitcast.97, s32[8192]{0:T(1024)S(1)} %get-tuple-element.156), kind=kCustom, calls=%fused_computation.2.clone | custom fusion | bytes 98304 | tf_op jit(solution)/shard_map/jit(_take)/gather | solution.py:70
  1203.2 45.5 %gather_fusion = f32[8192]{0:T(1024)S(1)} fusion(f32[32768]{0:T(1024)S(1)} %bitcast.98, s32[8192]{0:T(1024)S(1)} %get-tuple-element.155), kind=kCustom, calls=%fused_computation.clone | custom fusion | bytes 98304 | tf_op jit(solution)/shard_map/jit(_take)/gather | solution.py:69
  1249.4 37.4 %psum.29 = f32[]{:T(128)} all-reduce(f32[]{:T(128)} %get-tuple-element.133), channel_id=1, replica_groups=mesh['agent'=16,'grid'=2] {'agent'}, use_global_device_ids=true, to_apply=%region_12.15 | all-reduce | flops 1 | bytes 8 | tf_op jit(solution)/shard_map/psum | solution.py:128
  1287.5 2.7 fusion.64
  1290.2 45.5 %gather_fusion.7 = f32[8192]{0:T(1024)S(1)} fusion(f32[32768]{0:T(1024)S(1)} %bitcast.99, s32[8192]{0:T(1024)S(1)} %get-tuple-element.154), kind=kCustom, calls=%fused_computation.4.clone | custom fusion | bytes 98304 | tf_op jit(solution)/shard_map/jit(_take)/gather | solution.py:70
  1335.7 45.5 %gather_fusion.4 = f32[8192]{0:T(1024)S(1)} fusion(f32[32768]{0:T(1024)S(1)} %bitcast.100, s32[8192]{0:T(1024)S(1)} %get-tuple-element.153), kind=kCustom, calls=%fused_computation.3.clone | custom fusion | bytes 98304 | tf_op jit(solution)/shard_map/jit(_take)/gather | solution.py:69
  1381.9 39.2 %psum.30 = f32[]{:T(128)} all-reduce(f32[]{:T(128)} %get-tuple-element.131), channel_id=1, replica_groups=mesh['agent'=16,'grid'=2] {'agent'}, use_global_device_ids=true, to_apply=%region_14.17 | all-reduce | flops 1 | bytes 8 | tf_op jit(solution)/shard_map/psum | solution.py:128
  1421.7 2.7 fusion.62
  1424.5 45.5 %gather_fusion.11 = f32[8192]{0:T(1024)S(1)} fusion(f32[32768]{0:T(1024)S(1)} %bitcast.101, s32[8192]{0:T(1024)S(1)} %get-tuple-element.152), kind=kCustom, calls=%fused_computation.6.clone | custom fusion | bytes 98304 | tf_op jit(solution)/shard_map/jit(_take)/gather | solution.py:70
  1470.0 45.5 %gather_fusion.8 = f32[8192]{0:T(1024)S(1)} fusion(f32[32768]{0:T(1024)S(1)} %bitcast.102, s32[8192]{0:T(1024)S(1)} %get-tuple-element.151), kind=kCustom, calls=%fused_computation.5.clone | custom fusion | bytes 98304 | tf_op jit(solution)/shard_map/jit(_take)/gather | solution.py:69
  1516.2 37.2 %psum.31 = f32[]{:T(128)} all-reduce(f32[]{:T(128)} %get-tuple-element.129), channel_id=1, replica_groups=mesh['agent'=16,'grid'=2] {'agent'}, use_global_device_ids=true, to_apply=%region_16.19 | all-reduce | flops 1 | bytes 8 | tf_op jit(solution)/shard_map/psum | solution.py:128
  1555.1 45.5 %gather_fusion.15 = f32[8192]{0:T(1024)S(1)} fusion(f32[32768]{0:T(1024)S(1)} %bitcast.103, s32[8192]{0:T(1024)S(1)} %get-tuple-element.159), kind=kCustom, calls=%fused_computation.8.clone | custom fusion | bytes 98304 | tf_op jit(solution)/shard_map/jit(_take)/gather | solution.py:70
  1600.7 45.5 %gather_fusion.12 = f32[8192]{0:T(1024)S(1)} fusion(f32[32768]{0:T(1024)S(1)} %bitcast.104, s32[8192]{0:T(1024)S(1)} %get-tuple-element.160), kind=kCustom, calls=%fused_computation.7.clone | custom fusion | bytes 98304 | tf_op jit(solution)/shard_map/jit(_take)/gather | solution.py:69
  (1307 shorter events, 753.9 us)
Async XLA Ops:
  7.2 4.6 copy-start.7
  7.2 4.6 copy-start.8
  13.4 9.9 copy-start.5
  13.4 10.0 copy-start.6
  13.4 10.2 copy-start.9
  14.8 23.4 %all-to-all-start = ((f32[16,128,64]{1,2,0:T(8,128)}), f32[16,128,64]{1,2,0:T(8,128)S(1)}, u32[]{:S(2)}, u32[]{:S(2)}) async-start(f32[16,128,64]{1,2,0:T(8,128)} %copy.31), calls=%async_computation | async-start | bytes 1048576 | tf_op jit(solution)/shard_map/all_to_all | solution.py:106
  23.2 1121.4 %all-gather.2.cloned.1.call-start = ((), (), s32[]{:S(2)}) async-start(), calls=%async_computation.1 | async-start | bytes 8912896 | tf_op jit(solution)/shard_map/all_gather | solution.py:124
  38.5 792.2 %copy-start.3 = (f32[8192]{0:T(1024)S(1)}, f32[8192]{0:T(1024)}, u32[]{:S(2)}) copy-start(f32[8192]{0:T(1024)} %param.24) | copy-start | bytes 98308
  38.5 833.8 %copy-start.4 = (s32[4]{0:T(128)S(1)}, s32[4]{0:T(128)}, u32[]{:S(2)}) copy-start(s32[4]{0:T(128)} %param.27) | copy-start | bytes 52
  38.5 839.4 %copy-start.1 = (s32[4,8192]{1,0:T(4,128)S(1)}, s32[4,8192]{1,0:T(4,128)}, u32[]{:S(2)}) copy-start(s32[4,8192]{1,0:T(4,128)} %param.25) | copy-start | bytes 393220
  38.5 839.5 %copy-start.2 = (s32[4,8192]{1,0:T(4,128)S(1)}, s32[4,8192]{1,0:T(4,128)}, u32[]{:S(2)}) copy-start(s32[4,8192]{1,0:T(4,128)} %param.26) | copy-start | bytes 393220
  828.3 82.8 %copy-start = (f32[128,512]{1,0:T(8,128)}, f32[128,512]{1,0:T(8,128)S(1)}, u32[]{:S(2)}) copy-start(f32[128,512]{1,0:T(8,128)S(1)} %get-tuple-element.49) | copy-start | bytes 786436
Sparse Core Ops, SparseCore 0:
  830.8 110.8 all-gather.1
where the time goes:
time: 1670 us; the launch traced here: 1650 us
  local copies, waits for them, and re-layouts  970 us (58%)
  other arithmetic  464 us (28%)
  blocking collectives  157 us (9%)
  between operations  24.6 us (1%)
    gather x4, local copies, waits for them, and re-layouts, advance(): value_high = jnp.take(flattened, flat_index + 1)  182 us
    gather x4, local copies, waits for them, and re-layouts, advance(): value_low = jnp.take(flattened, flat_index)  182 us
    dynamic_update_slice x256, local copies, waits for them, and re-layouts, on_device(): values_now, policy = lax.map(one_state, (expected, growth, income))  177 us
    reduce_sum x128, other arithmetic, bellman(): chosen = jnp.sum(weight * points[None, :], axis=1) / totals  175 us
    add x128, other arithmetic, one_state(): return bellman(points, own_points * factor + earned, column)  166 us
    psum x4, blocking collectives, on_device(): capital = lax.psum(jnp.sum(current), 'agent') / agents_total  155 us
    dynamic_slice x256, local copies, waits for them, and re-layouts, on_device(): values_now, policy = lax.map(one_state, (expected, growth, income))  150 us
    gather x4, local copies, waits for them, and re-layouts, advance(): edge_high = jnp.take(points, bracket_row + 1)  132 us
  transfers between devices with their start and end apart: 2, of which 1 were waited for; matrix products, arithmetic and copies ran while one was open for 16% of the time, Pallas kernels for 0%

commit v1 on v0

v1 whole, which is shorter than its diff:
```python
import functools
import math
import jax
import jax.numpy as jnp
from jax import lax
from jax.experimental import pallas as pl
from jax.experimental.pallas import tpu as pltpu
from jax.sharding import PartitionSpec as P

wealth_upper_limit = 40.0
beta_disc = 0.96
tau_soft = 0.02
floor_cons = 0.1
highest = lax.Precision.HIGHEST
LOG2E = 1.0 / math.log(2.0)
SCALE = LOG2E / tau_soft
SLOPE = SCALE / floor_cons
JB = 32
IB = 8


def make_points(count):
    fraction = jnp.arange(count, dtype=jnp.float32) / (count - 1)
    return wealth_upper_limit * fraction * fraction


def hat_function_shares(position, knots):
    spacing = wealth_upper_limit / (knots - 1)
    mesh_points = wealth_upper_limit * jnp.arange(knots, dtype=jnp.float32) / (knots - 1)
    return jnp.maximum(0.0, 1.0 - jnp.abs(position[..., None] - mesh_points) / spacing)


def bellman_kernel(nlog_ref, nall_ref, score_ref, point_ref, wealth_ref, tail_m, tail_t, tail_q, tail_p,
                   value_ref, policy_ref, scratch):
    width = score_ref.shape[1]
    subs = JB // 8

    def group(g, _):
        row = pl.multiple_of(g * IB, IB)
        nlog = nlog_ref[g]
        nall = nall_ref[g]
        wealth = [jnp.broadcast_to(wealth_ref[pl.ds(row + r, 1), :], (8, width)) for r in range(IB)]

        def scores(block, tops, mixed):
            start = pl.multiple_of(block * JB, JB)
            tops = list(tops)
            for k in range(subs):
                at = pl.ds(start + 8 * k, 8)
                p = point_ref[at, :]
                e = score_ref[at, :]
                for r in range(IB):
                    c = wealth[r] - p
                    if mixed:
                        clipped = jnp.maximum(c, floor_cons)
                        s = jnp.log(clipped) * SCALE + ((c - clipped) * SLOPE + e)
                    else:
                        s = jnp.log(c) * SCALE + e
                    scratch[r, at, :] = s
                    tops[r] = jnp.maximum(tops[r], s)
            return tuple(tops)

        tops = tuple(jnp.full((8, width), -3e30, jnp.float32) for _ in range(IB))
        tops = lax.fori_loop(0, nlog, lambda b, t: scores(b, t, False), tops)
        tops = lax.fori_loop(nlog, nall, lambda b, t: scores(b, t, True), tops)
        edge = tail_p[pl.ds(nall, 1), :]
        ends = tail_m[pl.ds(nall, 1), :]
        rows = wealth_ref[pl.ds(row, IB), :]
        tail = (rows - edge) * SLOPE + (ends + SCALE * (math.log(floor_cons) - 1.0))
        top = jnp.concatenate([jnp.max(t, axis=0, keepdims=True) for t in tops], axis=0)
        top = jnp.maximum(top, tail)
        tops = [jnp.broadcast_to(top[r:r + 1, :], (8, width)) for r in range(IB)]

        def weigh(block, sums):
            start = pl.multiple_of(block * JB, JB)
            totals, moments = list(sums[0]), list(sums[1])
            for k in range(subs):
                at = pl.ds(start + 8 * k, 8)
                p = point_ref[at, :]
                for r in range(IB):
                    weight = jnp.exp2(scratch[r, at, :] - tops[r])
                    totals[r] = totals[r] + weight
                    moments[r] = moments[r] + weight * p
            return tuple(totals), tuple(moments)

        zero = tuple(jnp.zeros((8, width), jnp.float32) for _ in range(IB))
        totals, moments = lax.fori_loop(0, nall, weigh, (zero, zero))
        total = jnp.concatenate([jnp.sum(t, axis=0, keepdims=True) for t in totals], axis=0)
        moment = jnp.concatenate([jnp.sum(t, axis=0, keepdims=True) for t in moments], axis=0)
        share = jnp.exp2(tail - top)
        total = total + share * tail_t[pl.ds(nall, 1), :]
        moment = moment + share * tail_q[pl.ds(nall, 1), :]
        value_ref[pl.ds(row, IB), :] = (top * math.log(2.0) + jnp.log(total)) * tau_soft
        policy_ref[pl.ds(row, IB), :] = moment / total
        return 0

    lax.fori_loop(0, wealth_ref.shape[0] // IB, group, 0)


def bellman(points, own_points, growth, income, expected):
    count, width = expected.shape
    half = own_points.shape[0]
    wealth = own_points[:, None] * growth[None, :] + income[None, :]
    scaled = expected * (beta_disc * SCALE)
    grid_points = jnp.broadcast_to(points[:, None], (count, width))
    blocks = count // JB
    starts = points.reshape(blocks, JB)[:, 0]
    ends = points.reshape(blocks, JB)[:, -1]
    spans = wealth.reshape(half // IB, IB * width)
    nlog = jnp.sum(ends[None, :] <= jnp.min(spans, axis=1)[:, None] - floor_cons, axis=1, dtype=jnp.int32)
    nall = jnp.sum(starts[None, :] < jnp.max(spans, axis=1)[:, None] - floor_cons, axis=1, dtype=jnp.int32)
    local = points.reshape(blocks, JB) - starts[:, None]
    slope = scaled.reshape(blocks, JB, width) - SLOPE * local[:, :, None]
    block_m = jnp.max(slope, axis=1)
    block_w = jnp.exp2(slope - block_m[:, None, :])
    block_t = jnp.sum(block_w, axis=1)
    block_q = jnp.sum(block_w * points.reshape(blocks, JB, 1), axis=1)
    later = jnp.arange(blocks)[None, :] >= jnp.arange(blocks)[:, None]
    drop = jnp.where(later, SLOPE * (starts[None, :] - starts[:, None]), 1e30)
    shifted = block_m[None, :, :] - drop[:, :, None]
    tail_m = jnp.max(shifted, axis=1)
    share = jnp.exp2(shifted - tail_m[:, None, :])
    tail_t = jnp.sum(share * block_t[None], axis=1)
    tail_q = jnp.sum(share * block_q[None], axis=1)
    pad = ((0, 8), (0, 0))
    tail_m = jnp.pad(tail_m, pad, constant_values=-1e30)
    tail_t = jnp.pad(tail_t, pad)
    tail_q = jnp.pad(tail_q, pad)
    tail_p = jnp.pad(jnp.broadcast_to(starts[:, None], (blocks, width)), pad)
    vmem = pl.BlockSpec(memory_space=pltpu.VMEM)
    smem = pl.BlockSpec(memory_space=pltpu.SMEM)
    shape = jax.ShapeDtypeStruct((half, width), jnp.float32)
    return pl.pallas_call(
        bellman_kernel,
        out_shape=(shape, shape),
        in_specs=[smem, smem] + [vmem] * 7,
        out_specs=(vmem, vmem),
        scratch_shapes=[pltpu.VMEM((IB, count, width), jnp.float32)],
        name="bellman",
    )(nlog, nall, scaled, grid_points, wealth, tail_m, tail_t, tail_q, tail_p)


def advance_kernel(table_ref, held_ref, shock_ref, bracket_ref, out_ref, count):
    lanes = 128
    tiles = count // lanes
    groups = held_ref.shape[0] // 8
    low_row, low_lane, high_row, high_lane, shares = [], [], [], [], []
    for v in range(groups):
        at = slice(8 * v, 8 * v + 8)
        b = bracket_ref[at, :]
        e = shock_ref[at, :] * tiles
        low_row.append(e + b // lanes)
        low_lane.append(b % lanes)
        high_row.append(e + (b + 1) // lanes)
        high_lane.append((b + 1) % lanes)
        f0 = b.astype(jnp.float32) / (count - 1)
        f1 = (b + 1).astype(jnp.float32) / (count - 1)
        p0 = wealth_upper_limit * f0 * f0
        p1 = wealth_upper_limit * f1 * f1
        shares.append(jnp.clip((held_ref[at, :] - p0) / (p1 - p0), 0.0, 1.0))

    def step(r8, carry):
        lows, highs = list(carry[0]), list(carry[1])
        for q in range(8):
            r = r8 * 8 + q
            row = jnp.broadcast_to(table_ref[pl.ds(r, 1), :], (8, lanes))
            for v in range(groups):
                lows[v] = jnp.where(low_row[v] == r, jnp.take_along_axis(row, low_lane[v], axis=1), lows[v])
                highs[v] = jnp.where(high_row[v] == r, jnp.take_along_axis(row, high_lane[v], axis=1), highs[v])
        return tuple(lows), tuple(highs)

    zero = tuple(jnp.zeros((8, lanes), jnp.float32) for _ in range(groups))
    lows, highs = lax.fori_loop(0, table_ref.shape[0] // 8, step, (zero, zero))
    for v in range(groups):
        out_ref[8 * v:8 * v + 8, :] = lows[v] + shares[v] * (highs[v] - lows[v])


def advance(lookup, current, shock_row, bracket_row):
    kinds, count = lookup.shape
    table = lookup.reshape(kinds * count // 128, 128)
    vmem = pl.BlockSpec(memory_space=pltpu.VMEM)
    return pl.pallas_call(
        functools.partial(advance_kernel, count=count),
        out_shape=jax.ShapeDtypeStruct(current.shape, jnp.float32),
        in_specs=[vmem] * 4,
        out_specs=vmem,
        name="advance",
    )(table, current, shock_row, bracket_row)


def on_device(value_prior, trans_weight, perceived_law_coefficient, perceived_law_constant, interest,
              wage_level, efficiency, holdings, shocks, brackets, aggregate):
    zones, knots = interest.shape
    kinds = efficiency.shape[0]
    states = value_prior.shape[0]
    agent_count = lax.axis_size("agent")
    columns = value_prior.shape[1]
    count = columns * agent_count
    per_device = states // agent_count
    half = count // lax.axis_size("grid")
    first_state = lax.axis_index("agent") * per_device
    points = make_points(count)
    transition = trans_weight / jnp.sum(trans_weight, axis=1, keepdims=True)
    mesh_points = wealth_upper_limit * jnp.arange(knots, dtype=jnp.float32) / (knots - 1)
    predicted = jnp.clip(
        perceived_law_coefficient[:, None] * mesh_points[None, :] + perceived_law_constant[:, None],
        0.0, wealth_upper_limit)
    move = hat_function_shares(predicted, knots)
    cube = value_prior.T.reshape(columns, zones, knots, kinds)
    blended = jnp.einsum("nykf,zeyf->nzke", cube, transition.reshape(zones, kinds, zones, kinds), precision=highest)
    partial_value = jnp.einsum("zjk,nzke->nzje", move, blended, precision=highest).reshape(columns, states)
    expected = lax.all_to_all(partial_value, "agent", split_axis=1, concat_axis=0, tiled=True)
    growth_all = jnp.broadcast_to((1.0 + interest)[:, :, None], (zones, knots, kinds)).reshape(states)
    income_all = (wage_level[:, :, None] * efficiency[None, None, :]).reshape(states)
    growth = lax.dynamic_slice_in_dim(growth_all, first_state, per_device)
    income = lax.dynamic_slice_in_dim(income_all, first_state, per_device)
    own_points = lax.dynamic_slice_in_dim(points, lax.axis_index("grid") * half, half)
    value_t, policy_t = bellman(points, own_points, growth, income, expected)
    values_now, policy = value_t.T, policy_t.T
    agents_total = holdings.shape[0] * agent_count
    policy_cube = lax.all_gather(policy, "agent", axis=0, tiled=True).reshape(zones, knots, kinds, half)
    current = holdings.reshape(-1, 128)
    shock_rows = shocks.reshape(shocks.shape[0], -1, 128)
    bracket_rows = brackets.reshape(shocks.shape[0], -1, 128)
    capital_path = []
    for period in range(shocks.shape[0]):
        capital = lax.psum(jnp.sum(current), "agent") / agents_total
        capital_path.append(capital)
        knot_weights = hat_function_shares(capital, knots)
        sliced = lax.dynamic_index_in_dim(policy_cube, aggregate[period], 0, keepdims=False)
        own = jnp.sum(knot_weights[:, None, None] * sliced, axis=0)
        lookup = lax.all_gather(own, "grid", axis=1, tiled=True)
        current = advance(lookup, current, shock_rows[period], bracket_rows[period])
    return (values_now, policy, current.reshape(-1), jnp.stack(capital_path))


def solution(mesh):
    return jax.shard_map(
        on_device,
        mesh=mesh,
        in_specs=(P(None, "agent"), P(), P(), P(), P(), P(), P(), P("agent"), P(None, "agent"),
                  P(None, "agent"), P()),
        out_specs=(P("agent", "grid"), P("agent", "grid"), P("agent"), P()),
        check_vma=False,
    )
```

time: 1670 us -> 457 us (0.27)
  local copies, waits for them, and re-layouts: 970 us -> 19.1 us
  other arithmetic: 464 us -> 17.3 us
  Pallas kernels: 0 us -> 119 us
  waiting for transfers between devices: 14.5 us -> 91.6 us
    gather x16 -> x0, local copies, waits for them, and re-layouts: 627 us -> none  [the longest x4 182 us: advance(): value_high = jnp.take(flattened, flat_index + 1)]
    dynamic_update_slice x256 -> x0, local copies, waits for them, and re-layouts: 177 us -> none  [on_device(): values_now, policy = lax.map(one_state, (expected, growth, income))]
    reduce_sum x130 -> x8, other arithmetic: 176 us -> 7.61 us  [the longest x4 5.51 us: on_device(): own = jnp.sum(knot_weights[:, None, None] * sliced, axis=0)]
    add x130 -> x2, other arithmetic: 166 us -> 0.84 us  [the longest x1 0.84 us: bellman(): wealth = own_points[:, None] * growth[None, :] + income[None, :]]
    dynamic_slice x258 -> x3, local copies, waits for them, and re-layouts: 154 us -> 0.23 us  [the longest x1 0.08 us: on_device(): income = lax.dynamic_slice_in_dim(income_all, first_state, per_device)]
    pallas_call x0 -> x5, Pallas kernels: none -> 119 us  [the longest x4 61.3 us: advance(): pl.pallas_call(functools.partial(advance_kernel, count=count), out_shape=...]
    reduce_max x128 -> x2, other arithmetic: 113 us -> 1.35 us  [the longest x1 1.13 us: bellman(): jnp.max(spans, axis=1)[:, None] - floor_cons]
    all_gather x1, waiting for transfers between devices: 0.02 us -> 80.8 us  [on_device(): lax.all_gather(policy, 'agent', axis=0, tiled=True)]
  transfers between devices with their start and end apart: 2 -> 2, of which waited for: 1 -> 2; matrix products, arithmetic and copies ran while one was open for 16% -> 2% of each run, Pallas kernels for 0% -> 0%
where the time goes in v1:
time: 457 us; the launch traced here: 456 us
  blocking collectives  173 us (38%)
  Pallas kernels  119 us (26%)
  waiting for transfers between devices  91.6 us (20%)
  between operations  24.8 us (5%)
  local copies, waits for them, and re-layouts  19.1 us (4%)
  other arithmetic  17.3 us (4%)
  starting transfers between devices  8.38 us (2%)
    psum x4, blocking collectives, on_device(): capital = lax.psum(jnp.sum(current), 'agent') / agents_total  165 us
    all_gather x1, waiting for transfers between devices, on_device(): lax.all_gather(policy, 'agent', axis=0, tiled=True)  80.8 us
    pallas_call x4, Pallas kernels, advance(): pl.pallas_call(functools.partial(advance_kernel, count=count), out_shape=...  61.3 us
    pallas_call x1, Pallas kernels, bellman(): pl.pallas_call(bellman_kernel, out_shape=(shape, shape), in_specs=[smem,...  57.8 us
    all_to_all x1, waiting for transfers between devices, on_device(): lax.all_to_all(partial_value, 'agent', split_axis=1, concat_axis=0, tiled...  10.8 us
  transfers between devices with their start and end apart: 2, of which 2 were waited for; matrix products, arithmetic and copies ran while one was open for 2% of the time, Pallas kernels for 0%

profile of v1, /device:TPU:0, one launch (start us, length us, event | category | flops | bytes accessed | tf_op | source)
XLA Modules:
  0.0 456.1 jit_solution(12355781651738648486)
XLA Ops:
  7.2 1.4 copy.54
  8.6 0.9 reduce_sum.137
  9.5 0.9 broadcast_divide_fusion
  10.5 0.2 reshape.297
  10.7 1.1 convolution_bitcast_fusion.1
  11.8 0.1 add_clamp_fusion
  11.9 1.6 convolution_bitcast_fusion
  13.5 0.3 copy.58
  13.9 1.1 copy.59
  15.0 8.3 %all-to-all-start = ((f32[64,16,128]{2,0,1:T(8,128)}), f32[64,16,128]{2,0,1:T(8,128)S(1)}, u32[]{:S(2)}, u32[]{:S(2)}) async-start(f32[64,16,128]{2,0,1:T(8,128)} %copy.59), calls=%async_computation | async-start | bytes 1048576 | tf_op jit(solution)/shard_map/all_to_all | solution.py:211
  23.5 0.1 broadcast_multiply_fusion.1
  23.6 0.1 mul.235
  23.8 0.1 reshape.296
  23.8 0.1 dynamic_slice.24
  23.9 0.1 dynamic_slice.23
  24.0 0.1 dynamic_slice.22
  24.1 0.1 mul.227
  24.2 0.1 multiply_select_fusion
  24.4 1.1 fusion.15
  25.5 0.7 convert_reduce_fusion.nall_ref
  26.2 0.6 convert_reduce_fusion.1.nlog_ref
  26.8 0.8 multiply_add_fusion.wealth_ref
  27.6 10.8 %all-to-all-done = f32[64,16,128]{2,0,1:T(8,128)S(1)} async-done(((f32[64,16,128]{2,0,1:T(8,128)}), f32[64,16,128]{2,0,1:T(8,128)S(1)}, u32[]{:S(2)}, u32[]{:S(2)}) %all-to-all-start) | async-done | bytes 524320 | tf_op jit(solution)/shard_map/all_to_all | solution.py:211
  38.5 0.2 subtract_reduce_fusion.1
  38.7 0.5 multiply_reduce_fusion
  39.3 0.6 pad.16.tail_m
  39.9 0.3 fusion.12
  40.2 0.6 pad.17.tail_t
  40.8 0.6 pad.18.tail_q
  41.4 1.0 broadcast_in_dim.16.point_ref
  42.4 0.7 pad.20.tail_p
  43.1 57.8 %bellman.1 = (f32[512,128]{1,0:T(8,128)}, f32[512,128]{1,0:T(8,128)}) custom-call(s32[64]{0:T(128)} %convert_reduce_fusion.1.nlog_ref, s32[64]{0:T(128)} %convert_reduce_fusion.nall_ref, f32[1024,128]{1,0:T(8,128)} %bitcast.72, f32[1024,128]{1,0:T(8,128)} %broadcast_in_dim.16.point_ref, f32[512,128]{1,0:T(8,128)} %multiply_add_fusion.wealth_ref, ...), custom_call_target="tpu_custom_call" | custom-call | tf_op jit(solution)/shard_map/bellman/pallas_call | solution.py:132
  100.9 0.6 reduce_sum.142
  101.5 49.6 %psum.28 = f32[]{:T(128)} all-reduce(f32[]{:T(128)} %reduce_sum.142), channel_id=1, replica_groups=mesh['agent'=16,'grid'=2] {'agent'}, use_global_device_ids=true, to_apply=%region_12.13 | all-reduce | flops 1 | bytes 8 | tf_op jit(solution)/shard_map/psum | solution.py:226
  151.1 0.7 fusion.34
  159.5 0.7 fusion.33
  160.2 0.7 fusion.32
  161.0 80.8 %all-gather.2.cloned.1.call-done = f32[2048,512]{0,1:T(8,128)} async-done(((f32[128,512]{0,1:T(8,128)}), f32[2048,512]{0,1:T(8,128)}) %all-gather.2.cloned.1.call-update) | async-done | bytes 4194320 | tf_op jit(solution)/shard_map/all_gather | solution.py:220
  241.7 5.3 %copy.63 = f32[2048,512]{1,0:T(8,128)} copy(f32[2048,512]{0,1:T(8,128)} %all-gather.2.cloned.1.call-done) | data formatting | bytes 8388608 | tf_op jit(solution)/shard_map/all_gather | solution.py:220
  247.1 1.4 fusion.3
  248.5 1.9 all_gather.16
  250.4 0.7 reshape.300.table_ref
  251.1 15.3 %advance.4.held_ref = f32[64,128]{1,0:T(8,128)} custom-call(f32[256,128]{1,0:T(8,128)} %reshape.300.table_ref, f32[64,128]{1,0:T(8,128)} %bitcast.79, s32[64,128]{1,0:T(8,128)} %bitcast.86, s32[64,128]{1,0:T(8,128)} %bitcast.87), custom_call_target="tpu_custom_call" | custom-call | tf_op jit(solution)/shard_map/advance/pallas_call | solution.py:181
  266.4 1.4 reduce_sum.144
  268.5 39.5 %psum.29 = f32[]{:T(128)} all-reduce(f32[]{:T(128)} %reduce_sum.144), channel_id=1, replica_groups=mesh['agent'=16,'grid'=2] {'agent'}, use_global_device_ids=true, to_apply=%region_15.16 | all-reduce | flops 1 | bytes 8 | tf_op jit(solution)/shard_map/psum | solution.py:226
  308.7 1.4 fusion.2
  310.0 1.9 all_gather.17
  311.9 0.7 reshape.302.table_ref
  312.6 15.3 %advance.5.held_ref = f32[64,128]{1,0:T(8,128)} custom-call(f32[256,128]{1,0:T(8,128)} %reshape.302.table_ref, f32[64,128]{1,0:T(8,128)} %advance.4.held_ref, s32[64,128]{1,0:T(8,128)} %bitcast.84, s32[64,128]{1,0:T(8,128)} %bitcast.85), custom_call_target="tpu_custom_call" | custom-call | tf_op jit(solution)/shard_map/advance/pallas_call | solution.py:181
  327.9 1.4 reduce_sum.146
  329.3 0.8 copy.65
  330.2 37.2 %psum.30 = f32[]{:T(128)} all-reduce(f32[]{:T(128)} %reduce_sum.146), channel_id=1, replica_groups=mesh['agent'=16,'grid'=2] {'agent'}, use_global_device_ids=true, to_apply=%region_18.19 | all-reduce | flops 1 | bytes 8 | tf_op jit(solution)/shard_map/psum | solution.py:226
  368.0 1.4 fusion.1
  369.4 1.9 all_gather.18
  371.3 0.7 reshape.303.table_ref
  371.9 15.3 %advance.6.held_ref = f32[64,128]{1,0:T(8,128)} custom-call(f32[256,128]{1,0:T(8,128)} %reshape.303.table_ref, f32[64,128]{1,0:T(8,128)} %advance.5.held_ref, s32[64,128]{1,0:T(8,128)} %bitcast.82, s32[64,128]{1,0:T(8,128)} %bitcast.83), custom_call_target="tpu_custom_call" | custom-call | tf_op jit(solution)/shard_map/advance/pallas_call | solution.py:181
  387.3 1.4 reduce_sum.148
  388.6 0.8 copy.64
  389.5 39.2 %psum.31 = f32[]{:T(128)} all-reduce(f32[]{:T(128)} %reduce_sum.148), channel_id=1, replica_groups=mesh['agent'=16,'grid'=2] {'agent'}, use_global_device_ids=true, to_apply=%region_21.22 | all-reduce | flops 1 | bytes 8 | tf_op jit(solution)/shard_map/psum | solution.py:226
  429.3 1.4 fusion
  430.7 1.9 all_gather.19
  432.6 0.7 reshape.304.table_ref
  433.3 15.3 %advance.7 = f32[64,128]{1,0:T(8,128)} custom-call(f32[256,128]{1,0:T(8,128)} %reshape.304.table_ref, f32[64,128]{1,0:T(8,128)} %advance.6.held_ref, s32[64,128]{1,0:T(8,128)} %bitcast.80, s32[64,128]{1,0:T(8,128)} %bitcast.81), custom_call_target="tpu_custom_call" | custom-call | tf_op jit(solution)/shard_map/advance/pallas_call | solution.py:181
  448.6 0.6 pad_maximum_fusion
  (42 shorter events, 0.6 us)
Async XLA Ops:
  7.2 4.6 %copy-start.10 = (f32[4]{0:T(128)S(1)}, f32[4]{0:T(128)}, u32[]{:S(2)}) copy-start(f32[4]{0:T(128)} %param.14) | copy-start | bytes 52
  7.2 4.6 %copy-start.11 = (f32[4]{0:T(128)S(1)}, f32[4]{0:T(128)}, u32[]{:S(2)}) copy-start(f32[4]{0:T(128)} %param.13) | copy-start | bytes 52
  10.6 12.9 %copy-start.7 = (f32[4,16]{1,0:T(4,128)S(1)}, f32[4,16]{1,0:T(4,128)}, u32[]{:S(2)}) copy-start(f32[4,16]{1,0:T(4,128)} %param.16) | copy-start | bytes 772
  10.7 12.9 %copy-start.9 = (f32[32]{0:T(128)S(1)}, f32[32]{0:T(128)}, u32[]{:S(2)}) copy-start(f32[32]{0:T(128)} %param.17) | copy-start | bytes 388
  10.7 13.0 %copy-start.8 = (f32[4,16]{1,0:T(4,128)S(1)}, f32[4,16]{1,0:T(4,128)}, u32[]{:S(2)}) copy-start(f32[4,16]{1,0:T(4,128)} %param.15) | copy-start | bytes 772
  13.8 87.0 %copy-start.5 = (f32[8192]{0:T(1024)S(1)}, f32[8192]{0:T(1024)}, u32[]{:S(2)}) copy-start(f32[8192]{0:T(1024)} %param.18) | copy-start | bytes 98308
  13.9 137.2 %copy-start.6 = (s32[4]{0:T(128)S(1)}, s32[4]{0:T(128)}, u32[]{:S(2)}) copy-start(s32[4]{0:T(128)} %param.21) | copy-start | bytes 52
  13.9 145.7 %copy-start.3 = (s32[4,8192]{1,0:T(4,128)S(1)}, s32[4,8192]{1,0:T(4,128)}, u32[]{:S(2)}) copy-start(s32[4,8192]{1,0:T(4,128)} %param.19) | copy-start | bytes 393220
  13.9 146.4 %copy-start.4 = (s32[4,8192]{1,0:T(4,128)S(1)}, s32[4,8192]{1,0:T(4,128)}, u32[]{:S(2)}) copy-start(s32[4,8192]{1,0:T(4,128)} %param.20) | copy-start | bytes 393220
  15.0 23.4 %all-to-all-start = ((f32[64,16,128]{2,0,1:T(8,128)}), f32[64,16,128]{2,0,1:T(8,128)S(1)}, u32[]{:S(2)}, u32[]{:S(2)}) async-start(f32[64,16,128]{2,0,1:T(8,128)} %copy.59), calls=%async_computation | async-start | bytes 1048576 | tf_op jit(solution)/shard_map/all_to_all | solution.py:211
  23.4 218.4 %all-gather.2.cloned.1.call-start = ((), (), s32[]{:S(2)}) async-start(), calls=%async_computation.1 | async-start | bytes 4456448 | tf_op jit(solution)/shard_map/all_gather | solution.py:220
  38.5 4.6 %copy-start = (f32[64,16,128]{2,0,1:T(8,128)}, f32[64,16,128]{2,0,1:T(8,128)S(1)}, u32[]{:S(2)}) copy-start(f32[64,16,128]{2,0,1:T(8,128)S(1)} %broadcast_multiply_fusion) | copy-start | bytes 1572868
  161.0 168.4 %copy-start.1 = (f32[512,128]{1,0:T(8,128)S(1)}, f32[512,128]{1,0:T(8,128)}, u32[]{:S(2)}) copy-start(f32[512,128]{1,0:T(8,128)} %get-tuple-element.7) | copy-start | bytes 786436
  247.1 141.5 %copy-start.2 = (f32[512,128]{1,0:T(8,128)S(1)}, f32[512,128]{1,0:T(8,128)}, u32[]{:S(2)}) copy-start(f32[512,128]{1,0:T(8,128)} %get-tuple-element.6) | copy-start | bytes 786436
Sparse Core Ops, SparseCore 0:
  101.0 140.6 all-gather.1
